TPU v7x, 32 devices: a whole 2x2x4 slice. The times are simulated.
32 devices in a mesh: curve: 8 (over z, y), seg: 4 (over x, core).
Axes of the slice: x: 2, y: 2, z: 4, core: 2. Of those that a mesh axis runs over, the one named last changes fastest.
Arguments:
- solution: bfloat16 [16384, 128], P(('curve', 'seg')), may hold values from -6 to 6
- viscosity: float32 [131072], P(('curve', 'seg')), may hold values from 0.1 to 10
- slot_index: int32 [131072, 4], P(('curve', 'seg')), may hold values from 0 to 1279, as said below
- slot_weight: int32 [131072, 4], P(('curve', 'seg')), may hold values from -1 to 8, as said below
- mirror_rows: int32 [32, 4, 192], P(('curve', 'seg')), may hold values from 0 to 511
- ghost_live: int32 [32, 4], P(('curve', 'seg')), may hold values from 0 to 192, as said below
- cell_count: int32 [32], P(('curve', 'seg')), may hold values from 512 to 4096, as said below
- viscous_block: bfloat16 [128, 128], replicated, may hold values from -0.5 to 0.5
- pressure_block: bfloat16 [128, 128], replicated, may hold values from -0.5 to 0.5
Outputs:
- residual: float32 [16384, 128], P(('curve', 'seg'))
Inputs may be any that keep to these rules, and one draw needn't show every extreme that they name: `slot_index`: column 0 of each element is one of its device's owned blocks; other columns point to owned blocks or to ghost entries; ghost entries past a list's live count read zeros. `slot_weight`: each entry is one of -1, 3, 6, 8; column 0 is 8. `ghost_live`: some list is full in every draw. `cell_count`: some device is full in every draw; loads are skewed.
All inputs are finite; a program needn't handle non-finite values.
Results may differ from a plain program's by a relative error of at most 0.0035.
Values may be sent and summed in bfloat16 or wider, within the bound.
A program may use at most 64 MiB of HBM per device.

v0:
```python
import functools

import jax
import jax.numpy as jnp
from jax import lax
from jax.experimental import pallas as pl
from jax.experimental.pallas import tpu as pltpu
from jax.sharding import PartitionSpec as P

CHUNK = 1024
NN = (((1,), (0,)), ((), ()))
NT = (((1,), (1,)), ((), ()))
TN = (((0,), (0,)), ((), ()))


def shift_list(region_count):
    return [(region // 2 + 1) * (1 if region % 2 == 0 else -1) for region in range(region_count)]


def mul(left, right, dims=NN):
    return lax.dot_general(left, right, dims, preferred_element_type=jnp.float32)


def kernel(
    n_curve,
    n_seg,
    ghost_rows,
    region_count,
    sol_in,
    visc_in,
    index_in,
    code_in,
    mirror_in,
    live_in,
    count_ref,
    visc_mat_in,
    pres_mat_in,
    result_ref,
    sol_ref,
    visc_ref,
    index_ref,
    code_ref,
    mirror_ref,
    live_ref,
    visc_mat_ref,
    pres_mat_ref,
    load_sem,
    table,
    gathered,
    elem_out,
    mirror_table,
    out_ghost,
    in_ghost,
    out_part,
    in_part,
    send_sem,
    recv_sem,
    send_back_sem,
    recv_back_sem,
):
    pairs = (
        (mirror_in, mirror_ref),
        (live_in, live_ref),
        (sol_in, sol_ref),
        (index_in, index_ref),
        (code_in, code_ref),
        (visc_mat_in, visc_mat_ref),
        (pres_mat_in, pres_mat_ref),
        (visc_in, visc_ref),
    )
    loads = [
        pltpu.make_async_copy(source, target, load_sem.at[position])
        for position, (source, target) in enumerate(pairs)
    ]
    for load in loads:
        load.start()

    devices_all = n_curve * n_seg
    owned_rows, width = sol_ref.shape
    slot_total, elem_rows = index_ref.shape
    chunk = min(CHUNK, elem_rows)
    ghost_all = ghost_rows * region_count
    offsets = shift_list(region_count)
    me = lax.axis_index("curve") * n_seg + lax.axis_index("seg")

    def exists(other):
        return jnp.logical_and(other >= 0, other < devices_all)

    def place(other):
        safe = jnp.clip(other, 0, devices_all - 1)
        return (safe // n_seg, safe % n_seg)

    barrier = pltpu.get_barrier_semaphore()
    for offset in offsets:

        @pl.when(exists(me + offset))
        def _():
            pl.semaphore_signal(
                barrier,
                inc=1,
                device_id=place(me + offset),
                device_id_type=pl.DeviceIdType.MESH,
            )

    for load in loads[:3]:
        load.wait()

    lanes = lax.broadcasted_iota(jnp.int32, (1, ghost_rows), 1)
    rows32 = lax.broadcasted_iota(jnp.int32, (owned_rows, ghost_rows), 0)
    for region in range(region_count):
        listed = jnp.where(
            lanes < live_ref[0, region], mirror_ref[region : region + 1, :], -1
        )
        hit = rows32 == listed
        mirror_table[region] = jnp.where(hit, 1.0, 0.0).astype(jnp.bfloat16)
        out_ghost[pl.ds(region * ghost_rows, ghost_rows), :] = mul(
            mirror_table[region], sol_ref[...], TN
        ).astype(jnp.bfloat16)

    def ghost_copy(region, target):
        rows = pl.ds(region * ghost_rows, ghost_rows)
        return pltpu.make_async_remote_copy(
            src_ref=out_ghost.at[rows],
            dst_ref=in_ghost.at[rows],
            send_sem=send_sem.at[region],
            recv_sem=recv_sem.at[region],
            device_id=place(target),
            device_id_type=pl.DeviceIdType.MESH,
        )

    def part_copy(region, target):
        rows = pl.ds(region * ghost_rows, ghost_rows)
        return pltpu.make_async_remote_copy(
            src_ref=out_part.at[rows],
            dst_ref=in_part.at[rows],
            send_sem=send_back_sem.at[region],
            recv_sem=recv_back_sem.at[region],
            device_id=place(target),
            device_id_type=pl.DeviceIdType.MESH,
        )

    order = sorted(range(region_count), key=lambda region: -abs(offsets[region]))
    peers = sum(jnp.where(exists(me + offset), 1, 0) for offset in offsets)
    pl.semaphore_wait(barrier, peers)

    for region in order:

        @pl.when(exists(me + offsets[region]))
        def _():
            ghost_copy(region, me + offsets[region]).start()

    for region, offset in enumerate(offsets):
        rows = pl.ds(region * ghost_rows, ghost_rows)

        @pl.when(jnp.logical_not(exists(me - offset)))
        def _():
            in_ghost[rows, :] = jnp.zeros((ghost_rows, width), jnp.bfloat16)

        @pl.when(jnp.logical_not(exists(me + offset)))
        def _():
            in_part[rows, :] = jnp.zeros((ghost_rows, width), jnp.bfloat16)

    for load in loads[3:]:
        load.wait()

    both = jnp.concatenate(
        [
            visc_mat_ref[...].astype(jnp.float32).T.astype(jnp.bfloat16),
            pres_mat_ref[...].astype(jnp.float32).T.astype(jnp.bfloat16),
        ],
        axis=0,
    )
    owned_values = mul(both, sol_ref[...], NT).astype(jnp.bfloat16)

    group = 16

    def table_rows(start, total, indices, weights):
        shape = (total // group, group, chunk)
        position = (
            lax.broadcasted_iota(jnp.int32, shape, 0) * group
            + lax.broadcasted_iota(jnp.int32, shape, 1)
            + start
        ).astype(jnp.int16)
        zero = jnp.zeros(shape, jnp.bfloat16)
        value = None
        for index, weight in zip(indices, weights):
            hit = position == jnp.broadcast_to(index[None], shape)
            part = jnp.where(hit, jnp.broadcast_to(weight[None], shape), zero)
            value = part if value is None else value + part
        return value.reshape(total, chunk)

    block = 64

    def build(step, carry):
        first = pl.multiple_of(step * chunk, chunk)
        columns = pl.ds(first, chunk)
        element = lax.broadcasted_iota(jnp.int32, (1, chunk), 1) + first
        alive = element < count_ref[0]
        indices, weights = [], []
        for slot in range(slot_total):
            index = index_ref[slot : slot + 1, columns]
            code = code_ref[slot : slot + 1, columns].astype(jnp.float32) * 0.125
            weight = jnp.where(alive, code, 0.0)
            indices.append(jnp.broadcast_to(index, (group, chunk)).astype(jnp.int16))
            weights.append(jnp.broadcast_to(weight, (group, chunk)).astype(jnp.bfloat16))
        for start in range(0, owned_rows, block):
            table[pl.ds(start, block), columns] = table_rows(start, block, indices, weights)
        gathered[:, columns] = mul(owned_values, table[pl.ds(0, owned_rows), columns])
        for start in range(owned_rows, owned_rows + ghost_all, block):
            table[pl.ds(start, block), columns] = table_rows(
                start, block, indices[1:], weights[1:]
            )
        return carry

    lax.fori_loop(0, elem_rows // chunk, build, 0)

    for region, offset in enumerate(offsets):

        @pl.when(exists(me - offset))
        def _():
            ghost_copy(region, me - offset).wait_recv()

    ghost_values = mul(both, in_ghost[...], NT).astype(jnp.bfloat16)

    def apply(step, carry):
        columns = pl.ds(pl.multiple_of(step * chunk, chunk), chunk)
        total = gathered[:, columns] + mul(
            ghost_values, table[pl.ds(owned_rows, ghost_all), columns]
        )
        value = visc_ref[:, columns] * total[:width] + total[width:]
        elem_out[columns, :] = value.T.astype(jnp.bfloat16)
        return carry

    lax.fori_loop(0, elem_rows // chunk, apply, 0)

    for region in order:
        offset = offsets[region]
        rows = pl.ds(region * ghost_rows, ghost_rows)
        out_part[rows, :] = mul(
            table[pl.ds(owned_rows + region * ghost_rows, ghost_rows), :], elem_out[...]
        ).astype(jnp.bfloat16)

        @pl.when(exists(me - offset))
        def _():
            part_copy(region, me - offset).start()

    result_ref[...] = mul(table[pl.ds(0, owned_rows), :], elem_out[...])

    for region, offset in enumerate(offsets):

        @pl.when(exists(me + offset))
        def _():
            part_copy(region, me + offset).wait_recv()

    total = result_ref[...]
    for region in range(region_count):
        total = total + mul(
            mirror_table[region], in_part[pl.ds(region * ghost_rows, ghost_rows), :]
        )
    result_ref[...] = total

    for region, offset in enumerate(offsets):

        @pl.when(exists(me + offset))
        def _():
            ghost_copy(region, me + offset).wait_send()

        @pl.when(exists(me - offset))
        def _():
            part_copy(region, me - offset).wait_send()


def per_device(
    n_curve,
    n_seg,
    solution,
    viscosity,
    slot_index,
    slot_weight,
    mirror_rows,
    ghost_live,
    cell_count,
    viscous_block,
    pressure_block,
):
    owned_rows, width = solution.shape
    region_count, ghost_rows = mirror_rows.shape[1:]
    elem_rows = viscosity.shape[0]
    ghost_all = region_count * ghost_rows
    column_total = owned_rows + ghost_all
    vmem = pl.BlockSpec(memory_space=pltpu.VMEM)
    hbm = pl.BlockSpec(memory_space=pltpu.HBM)
    smem = pl.BlockSpec(memory_space=pltpu.SMEM)
    ghost_buffer = pltpu.VMEM((ghost_all, width), jnp.bfloat16)
    semaphores = pltpu.SemaphoreType.DMA((region_count,))
    return pl.pallas_call(
        functools.partial(kernel, n_curve, n_seg, ghost_rows, region_count),
        out_shape=jax.ShapeDtypeStruct((owned_rows, width), jnp.float32),
        in_specs=[hbm] * 6 + [smem] + [hbm] * 2,
        out_specs=vmem,
        scratch_shapes=[
            pltpu.VMEM(solution.shape, solution.dtype),
            pltpu.VMEM((1, elem_rows), viscosity.dtype),
            pltpu.VMEM(slot_index.shape[::-1], slot_index.dtype),
            pltpu.VMEM(slot_weight.shape[::-1], slot_weight.dtype),
            pltpu.VMEM(mirror_rows.shape[1:], mirror_rows.dtype),
            pltpu.SMEM(ghost_live.shape, ghost_live.dtype),
            pltpu.VMEM(viscous_block.shape, viscous_block.dtype),
            pltpu.VMEM(pressure_block.shape, pressure_block.dtype),
            pltpu.SemaphoreType.DMA((8,)),
            pltpu.VMEM((column_total, elem_rows), jnp.bfloat16),
            pltpu.VMEM((2 * width, elem_rows), jnp.float32),
            pltpu.VMEM((elem_rows, width), jnp.bfloat16),
            pltpu.VMEM((region_count, owned_rows, ghost_rows), jnp.bfloat16),
            ghost_buffer,
            ghost_buffer,
            ghost_buffer,
            ghost_buffer,
            semaphores,
            semaphores,
            semaphores,
            semaphores,
        ],
        compiler_params=pltpu.CompilerParams(
            collective_id=0, has_side_effects=True, vmem_limit_bytes=60 * 1024 * 1024
        ),
        name="stokes_operator",
    )(
        solution,
        viscosity.reshape(1, elem_rows),
        slot_index.T,
        slot_weight.T,
        mirror_rows[0],
        ghost_live,
        cell_count,
        viscous_block,
        pressure_block,
    )


def solution(mesh):
    return jax.shard_map(
        functools.partial(per_device, mesh.shape["curve"], mesh.shape["seg"]),
        mesh=mesh,
        in_specs=(
            P(("curve", "seg"), None),
            P(("curve", "seg")),
            P(("curve", "seg"), None),
            P(("curve", "seg"), None),
            P(("curve", "seg"), None, None),
            P(("curve", "seg"), None),
            P(("curve", "seg")),
            P(),
            P(),
        ),
        out_specs=P(("curve", "seg"), None),
        check_vma=False,
    )
```

profile of v0, /device:TPU:1, one launch (start us, length us, event | category | flops | bytes accessed | tf_op | source)
XLA Modules:
  0.0 20.9 jit_solution(16640307433838646071)
XLA Ops:
  0.7 18.5 %stokes_operator.1 = f32[512,128]{1,0:T(8,128)} custom-call(bf16[512,128]{1,0:T(8,128)(2,1)} %sol_in.1, f32[1,4096]{1,0:T(1,128)} %bitcast.6, s32[4,4096]{1,0:T(4,128)} %bitcast.4, s32[4,4096]{1,0:T(4,128)} %bitcast.5, s32[4,192]{1,0:T(4,128)} %bitcast.7, s32[1,4]{1,0:T(1,128)} %live_in.1, s32[1]{0:T(128)S(6)} %copy.11.count_ref, ...), custom_call_target="tpu_custom_call" | custom-call | tf_op jit(solution)/shard_map/stokes_operator/pallas_call | solution.py:296
  19.2 1.7 %copy.12 = f32[512,128]{1,0:T(8,128)} copy(f32[512,128]{1,0:T(8,128)} %stokes_operator.1) | data formatting | bytes 524288
where the time goes:
time: 21.1 us; the launch traced here: 20.9 us
  Pallas kernels  18.5 us (88%)
  local copies, waits for them, and re-layouts  1.67 us (8%)
  between operations  0.66 us (3%)
    pallas_call x1, Pallas kernels, per_device(): pl.pallas_call(functools.partial(kernel, n_curve, n_seg, ghost_rows, regi...  18.5 us
    unnamed x1, local copies, waits for them, and re-layouts  1.67 us

commit v1 on v0

--- a/solution.py
+++ b/solution.py
@@ -8,6 +8,8 @@
 from jax.sharding import PartitionSpec as P
 
 CHUNK = 1024
+GROUP = 16
+BLOCK = 64
 NN = (((1,), (0,)), ((), ()))
 NT = (((1,), (1,)), ((), ()))
 TN = (((0,), (0,)), ((), ()))
@@ -32,7 +34,7 @@
     code_in,
     mirror_in,
     live_in,
-    count_ref,
+    count_in,
     visc_mat_in,
     pres_mat_in,
     result_ref,
@@ -44,7 +46,10 @@
     live_ref,
     visc_mat_ref,
     pres_mat_ref,
+    count_ref,
     load_sem,
+    sol_flip,
+    local,
     table,
     gathered,
     elem_out,
@@ -62,6 +67,7 @@
         (mirror_in, mirror_ref),
         (live_in, live_ref),
         (sol_in, sol_ref),
+        (count_in, count_ref),
         (index_in, index_ref),
         (code_in, code_ref),
         (visc_mat_in, visc_mat_ref),
@@ -105,17 +111,26 @@
     for load in loads[:3]:
         load.wait()
 
+    order = sorted(range(region_count), key=lambda region: -abs(offsets[region]))
+    sol_flip[...] = sol_ref[...].T
+
     lanes = lax.broadcasted_iota(jnp.int32, (1, ghost_rows), 1)
-    rows32 = lax.broadcasted_iota(jnp.int32, (owned_rows, ghost_rows), 0)
-    for region in range(region_count):
+    shape = (owned_rows // GROUP, GROUP, ghost_rows)
+    position = (
+        lax.broadcasted_iota(jnp.int32, shape, 0) * GROUP
+        + lax.broadcasted_iota(jnp.int32, shape, 1)
+    ).astype(jnp.int16)
+    for region in order:
         listed = jnp.where(
             lanes < live_ref[0, region], mirror_ref[region : region + 1, :], -1
         )
-        hit = rows32 == listed
-        mirror_table[region] = jnp.where(hit, 1.0, 0.0).astype(jnp.bfloat16)
+        listed = jnp.broadcast_to(listed, (GROUP, ghost_rows)).astype(jnp.int16)
+        hit = position == jnp.broadcast_to(listed[None], shape)
+        chosen = jnp.where(hit, jnp.ones(shape, jnp.bfloat16), jnp.zeros(shape, jnp.bfloat16))
+        mirror_table[region] = chosen.reshape(owned_rows, ghost_rows)
         out_ghost[pl.ds(region * ghost_rows, ghost_rows), :] = mul(
-            mirror_table[region], sol_ref[...], TN
-        ).astype(jnp.bfloat16)
+            sol_flip[...], mirror_table[region]
+        ).T.astype(jnp.bfloat16)
 
     def ghost_copy(region, target):
         rows = pl.ds(region * ghost_rows, ghost_rows)
@@ -139,7 +154,6 @@
             device_id_type=pl.DeviceIdType.MESH,
         )
 
-    order = sorted(range(region_count), key=lambda region: -abs(offsets[region]))
     peers = sum(jnp.where(exists(me + offset), 1, 0) for offset in offsets)
     pl.semaphore_wait(barrier, peers)
 
@@ -163,101 +177,104 @@
     for load in loads[3:]:
         load.wait()
 
-    both = jnp.concatenate(
+    applied = jnp.concatenate(
         [
             visc_mat_ref[...].astype(jnp.float32).T.astype(jnp.bfloat16),
             pres_mat_ref[...].astype(jnp.float32).T.astype(jnp.bfloat16),
         ],
-        axis=0,
+        axis=1,
     )
-    owned_values = mul(both, sol_ref[...], NT).astype(jnp.bfloat16)
-
-    group = 16
 
     def table_rows(start, total, indices, weights):
-        shape = (total // group, group, chunk)
+        shape = (total // GROUP, GROUP, chunk)
         position = (
-            lax.broadcasted_iota(jnp.int32, shape, 0) * group
+            lax.broadcasted_iota(jnp.int32, shape, 0) * GROUP
             + lax.broadcasted_iota(jnp.int32, shape, 1)
             + start
         ).astype(jnp.int16)
-        zero = jnp.zeros(shape, jnp.bfloat16)
-        value = None
+        value = jnp.zeros(shape, jnp.bfloat16)
         for index, weight in zip(indices, weights):
             hit = position == jnp.broadcast_to(index[None], shape)
-            part = jnp.where(hit, jnp.broadcast_to(weight[None], shape), zero)
-            value = part if value is None else value + part
+            value = jnp.where(hit, jnp.broadcast_to(weight[None], shape), value)
         return value.reshape(total, chunk)
 
-    block = 64
-
-    def build(step, carry):
-        first = pl.multiple_of(step * chunk, chunk)
-        columns = pl.ds(first, chunk)
-        element = lax.broadcasted_iota(jnp.int32, (1, chunk), 1) + first
+    chunks = [pl.ds(first, chunk) for first in range(0, elem_rows, chunk)]
+
+    for step, columns in enumerate(chunks):
+        element = lax.broadcasted_iota(jnp.int32, (1, chunk), 1) + step * chunk
         alive = element < count_ref[0]
         indices, weights = [], []
         for slot in range(slot_total):
             index = index_ref[slot : slot + 1, columns]
             code = code_ref[slot : slot + 1, columns].astype(jnp.float32) * 0.125
             weight = jnp.where(alive, code, 0.0)
-            indices.append(jnp.broadcast_to(index, (group, chunk)).astype(jnp.int16))
-            weights.append(jnp.broadcast_to(weight, (group, chunk)).astype(jnp.bfloat16))
-        for start in range(0, owned_rows, block):
-            table[pl.ds(start, block), columns] = table_rows(start, block, indices, weights)
-        gathered[:, columns] = mul(owned_values, table[pl.ds(0, owned_rows), columns])
-        for start in range(owned_rows, owned_rows + ghost_all, block):
-            table[pl.ds(start, block), columns] = table_rows(
-                start, block, indices[1:], weights[1:]
+            indices.append(jnp.broadcast_to(index, (GROUP, chunk)).astype(jnp.int16))
+            weights.append(jnp.broadcast_to(weight, (GROUP, chunk)).astype(jnp.bfloat16))
+        sums = []
+        for slot in range(slot_total):
+            value = weights[slot]
+            for other in range(slot):
+                same = indices[other] == indices[slot]
+                value = value + jnp.where(same, weights[other], jnp.zeros_like(value))
+            sums.append(value)
+        for start in range(0, owned_rows, BLOCK):
+            table[pl.ds(start, BLOCK), columns] = table_rows(start, BLOCK, indices, sums)
+        gathered[:, columns] = mul(sol_flip[...], table[pl.ds(0, owned_rows), columns])
+        for start in range(owned_rows, owned_rows + ghost_all, BLOCK):
+            table[pl.ds(start, BLOCK), columns] = table_rows(
+                start, BLOCK, indices[1:], sums[1:]
             )
-        return carry
-
-    lax.fori_loop(0, elem_rows // chunk, build, 0)
-
-    for region, offset in enumerate(offsets):
+
+    for turn, region in enumerate(order):
+        offset = offsets[region]
 
         @pl.when(exists(me - offset))
         def _():
             ghost_copy(region, me - offset).wait_recv()
 
-    ghost_values = mul(both, in_ghost[...], NT).astype(jnp.bfloat16)
-
-    def apply(step, carry):
-        columns = pl.ds(pl.multiple_of(step * chunk, chunk), chunk)
-        total = gathered[:, columns] + mul(
-            ghost_values, table[pl.ds(owned_rows, ghost_all), columns]
-        )
-        value = visc_ref[:, columns] * total[:width] + total[width:]
-        elem_out[columns, :] = value.T.astype(jnp.bfloat16)
-        return carry
-
-    lax.fori_loop(0, elem_rows // chunk, apply, 0)
+        rows = pl.ds(region * ghost_rows, ghost_rows)
+        flipped = in_ghost[rows, :].T
+        for columns in chunks:
+            value = gathered[:, columns] + mul(
+                flipped, table[pl.ds(owned_rows + region * ghost_rows, ghost_rows), columns]
+            )
+            if turn < region_count - 1:
+                gathered[:, columns] = value
+            else:
+                element = value.astype(jnp.bfloat16)
+                scaled = (element.astype(jnp.float32) * visc_ref[:, columns]).astype(jnp.bfloat16)
+                pair = jnp.concatenate([scaled, element], axis=0)
+                elem_out[:, columns] = mul(applied, pair).astype(jnp.bfloat16)
 
     for region in order:
         offset = offsets[region]
         rows = pl.ds(region * ghost_rows, ghost_rows)
         out_part[rows, :] = mul(
-            table[pl.ds(owned_rows + region * ghost_rows, ghost_rows), :], elem_out[...]
-        ).astype(jnp.bfloat16)
+            elem_out[...],
+            table[pl.ds(owned_rows + region * ghost_rows, ghost_rows), :],
+            NT,
+        ).T.astype(jnp.bfloat16)
 
         @pl.when(exists(me - offset))
         def _():
             part_copy(region, me - offset).start()
 
-    result_ref[...] = mul(table[pl.ds(0, owned_rows), :], elem_out[...])
-
-    for region, offset in enumerate(offsets):
+    local[...] = mul(elem_out[...], table[pl.ds(0, owned_rows), :], NT).T
+
+    for region in order:
+        offset = offsets[region]
 
         @pl.when(exists(me + offset))
         def _():
             part_copy(region, me + offset).wait_recv()
 
-    total = result_ref[...]
-    for region in range(region_count):
-        total = total + mul(
+        value = local[...] + mul(
             mirror_table[region], in_part[pl.ds(region * ghost_rows, ghost_rows), :]
         )
-    result_ref[...] = total
+        if region == order[-1]:
+            result_ref[...] = value
+        else:
+            local[...] = value
 
     for region, offset in enumerate(offsets):
 
@@ -290,13 +307,12 @@
     column_total = owned_rows + ghost_all
     vmem = pl.BlockSpec(memory_space=pltpu.VMEM)
     hbm = pl.BlockSpec(memory_space=pltpu.HBM)
-    smem = pl.BlockSpec(memory_space=pltpu.SMEM)
     ghost_buffer = pltpu.VMEM((ghost_all, width), jnp.bfloat16)
     semaphores = pltpu.SemaphoreType.DMA((region_count,))
     return pl.pallas_call(
         functools.partial(kernel, n_curve, n_seg, ghost_rows, region_count),
-        out_shape=jax.ShapeDtypeStruct((owned_rows, width), jnp.float32),
-        in_specs=[hbm] * 6 + [smem] + [hbm] * 2,
+        out_shape=pltpu.VMEM((owned_rows, width), jnp.float32),
+        in_specs=[hbm] * 9,
         out_specs=vmem,
         scratch_shapes=[
             pltpu.VMEM(solution.shape, solution.dtype),
@@ -307,10 +323,13 @@
             pltpu.SMEM(ghost_live.shape, ghost_live.dtype),
             pltpu.VMEM(viscous_block.shape, viscous_block.dtype),
             pltpu.VMEM(pressure_block.shape, pressure_block.dtype),
-            pltpu.SemaphoreType.DMA((8,)),
+            pltpu.SMEM(cell_count.shape, cell_count.dtype),
+            pltpu.SemaphoreType.DMA((9,)),
+            pltpu.VMEM((width, owned_rows), jnp.bfloat16),
+            pltpu.VMEM((owned_rows, width), jnp.float32),
             pltpu.VMEM((column_total, elem_rows), jnp.bfloat16),
-            pltpu.VMEM((2 * width, elem_rows), jnp.float32),
-            pltpu.VMEM((elem_rows, width), jnp.bfloat16),
+            pltpu.VMEM((width, elem_rows), jnp.float32),
+            pltpu.VMEM((width, elem_rows), jnp.bfloat16),
             pltpu.VMEM((region_count, owned_rows, ghost_rows), jnp.bfloat16),
             ghost_buffer,
             ghost_buffer,

time: 21.1 us -> 18.8 us (0.89)
  Pallas kernels: 18.5 us -> 17.2 us
  local copies, waits for them, and re-layouts: 1.67 us -> 0.71 us
    pallas_call x1, Pallas kernels: 18.5 us -> 17.2 us  [per_device(): pl.pallas_call(functools.partial(kernel, n_curve, n_seg, ghost_rows, regi...]
    unnamed x1, local copies, waits for them, and re-layouts: 1.67 us -> 0.71 us
where the time goes in v1:
time: 18.8 us; the launch traced here: 18.6 us
  Pallas kernels  17.2 us (91%)
  local copies, waits for them, and re-layouts  0.71 us (4%)
  between operations  0.66 us (4%)
    pallas_call x1, Pallas kernels, per_device(): pl.pallas_call(functools.partial(kernel, n_curve, n_seg, ghost_rows, regi...  17.2 us
    unnamed x1, local copies, waits for them, and re-layouts  0.71 us

profile of v1, /device:TPU:1, one launch (start us, length us, event | category | flops | bytes accessed | tf_op | source)
XLA Modules:
  0.0 18.6 jit_solution(4349097597716844878)
XLA Ops:
  0.7 17.2 %stokes_operator.1 = f32[512,128]{1,0:T(8,128)S(1)} custom-call(bf16[512,128]{1,0:T(8,128)(2,1)} %sol_in.1, f32[1,4096]{1,0:T(1,128)} %bitcast.6, s32[4,4096]{1,0:T(4,128)} %bitcast.4, s32[4,4096]{1,0:T(4,128)} %bitcast.5, s32[4,192]{1,0:T(4,128)} %bitcast.7, s32[1,4]{1,0:T(1,128)} %live_in.1, s32[1]{0:T(128)S(6)} %copy.12.count_in, ...), custom_call_target="tpu_custom_call" | custom-call | tf_op jit(solution)/shard_map/stokes_operator/pallas_call | solution.py:312
  17.9 0.7 %copy.11 = f32[512,128]{1,0:T(8,128)} copy(f32[512,128]{1,0:T(8,128)S(1)} %stokes_operator.1) | data formatting | bytes 524288

commit v2 on v1

--- a/solution.py
+++ b/solution.py
@@ -51,6 +51,7 @@
     sol_flip,
     local,
     table,
+    table_flip,
     gathered,
     elem_out,
     mirror_table,
@@ -111,7 +112,6 @@
     for load in loads[:3]:
         load.wait()
 
-    order = sorted(range(region_count), key=lambda region: -abs(offsets[region]))
     sol_flip[...] = sol_ref[...].T
 
     lanes = lax.broadcasted_iota(jnp.int32, (1, ghost_rows), 1)
@@ -120,7 +120,7 @@
         lax.broadcasted_iota(jnp.int32, shape, 0) * GROUP
         + lax.broadcasted_iota(jnp.int32, shape, 1)
     ).astype(jnp.int16)
-    for region in order:
+    for region in range(region_count):
         listed = jnp.where(
             lanes < live_ref[0, region], mirror_ref[region : region + 1, :], -1
         )
@@ -132,8 +132,24 @@
             sol_flip[...], mirror_table[region]
         ).T.astype(jnp.bfloat16)
 
+    def offset_of(region):
+        return (region // 2 + 1) * (1 - 2 * (region % 2))
+
+    def part_rows(region):
+        return pl.ds(pl.multiple_of(region * ghost_rows, GROUP), ghost_rows)
+
+    edge = me < n_seg
+
+    def send_order(step_of):
+        near = sorted(range(region_count), key=lambda region: (abs(step_of(region)), step_of(region)))
+        down = sorted(range(region_count), key=step_of)
+        return near, [jnp.where(edge, first, other) for first, other in zip(down, near)]
+
+    near_order, order = send_order(lambda region: offsets[region])
+    back_near, back_order = send_order(lambda region: -offsets[region])
+
     def ghost_copy(region, target):
-        rows = pl.ds(region * ghost_rows, ghost_rows)
+        rows = part_rows(region)
         return pltpu.make_async_remote_copy(
             src_ref=out_ghost.at[rows],
             dst_ref=in_ghost.at[rows],
@@ -144,7 +160,7 @@
         )
 
     def part_copy(region, target):
-        rows = pl.ds(region * ghost_rows, ghost_rows)
+        rows = part_rows(region)
         return pltpu.make_async_remote_copy(
             src_ref=out_part.at[rows],
             dst_ref=in_part.at[rows],
@@ -159,9 +175,9 @@
 
     for region in order:
 
-        @pl.when(exists(me + offsets[region]))
-        def _():
-            ghost_copy(region, me + offsets[region]).start()
+        @pl.when(exists(me + offset_of(region)))
+        def _():
+            ghost_copy(region, me + offset_of(region)).start()
 
     for region, offset in enumerate(offsets):
         rows = pl.ds(region * ghost_rows, ghost_rows)
@@ -224,57 +240,55 @@
             table[pl.ds(start, BLOCK), columns] = table_rows(
                 start, BLOCK, indices[1:], sums[1:]
             )
-
-    for turn, region in enumerate(order):
-        offset = offsets[region]
-
-        @pl.when(exists(me - offset))
-        def _():
-            ghost_copy(region, me - offset).wait_recv()
-
-        rows = pl.ds(region * ghost_rows, ghost_rows)
-        flipped = in_ghost[rows, :].T
-        for columns in chunks:
-            value = gathered[:, columns] + mul(
-                flipped, table[pl.ds(owned_rows + region * ghost_rows, ghost_rows), columns]
-            )
-            if turn < region_count - 1:
-                gathered[:, columns] = value
-            else:
-                element = value.astype(jnp.bfloat16)
-                scaled = (element.astype(jnp.float32) * visc_ref[:, columns]).astype(jnp.bfloat16)
-                pair = jnp.concatenate([scaled, element], axis=0)
-                elem_out[:, columns] = mul(applied, pair).astype(jnp.bfloat16)
-
-    for region in order:
-        offset = offsets[region]
-        rows = pl.ds(region * ghost_rows, ghost_rows)
-        out_part[rows, :] = mul(
-            elem_out[...],
-            table[pl.ds(owned_rows + region * ghost_rows, ghost_rows), :],
-            NT,
-        ).T.astype(jnp.bfloat16)
-
-        @pl.when(exists(me - offset))
-        def _():
-            part_copy(region, me - offset).start()
+        for region in range(region_count):
+            first = owned_rows + region * ghost_rows
+            table_flip[region, columns, :] = table[pl.ds(first, ghost_rows), columns].T
+
+    values = [gathered[:, columns] for columns in chunks]
+    for region in near_order:
+
+        @pl.when(exists(me - offset_of(region)))
+        def _():
+            ghost_copy(region, me - offset_of(region)).wait_recv()
+
+        flipped = in_ghost[part_rows(region), :].T
+        first = owned_rows + region * ghost_rows
+        values = [
+            value + mul(flipped, table[pl.ds(first, ghost_rows), columns])
+            for value, columns in zip(values, chunks)
+        ]
+    pairs = []
+    for value, columns in zip(values, chunks):
+        element = value.astype(jnp.bfloat16)
+        scaled = (element.astype(jnp.float32) * visc_ref[:, columns]).astype(jnp.bfloat16)
+        pairs.append(jnp.concatenate([scaled, element], axis=0))
+    for pair, columns in zip(pairs, chunks):
+        elem_out[:, columns] = mul(applied, pair).astype(jnp.bfloat16)
+
+    for group in (back_order[:2], back_order[2:]):
+        parts = [mul(elem_out[...], table_flip[region]) for region in group]
+        for region, part in zip(group, parts):
+            out_part[part_rows(region), :] = part.T.astype(jnp.bfloat16)
+        for region in group:
+
+            @pl.when(exists(me - offset_of(region)))
+            def _():
+                part_copy(region, me - offset_of(region)).start()
 
     local[...] = mul(elem_out[...], table[pl.ds(0, owned_rows), :], NT).T
 
-    for region in order:
-        offset = offsets[region]
-
-        @pl.when(exists(me + offset))
-        def _():
-            part_copy(region, me + offset).wait_recv()
-
-        value = local[...] + mul(
-            mirror_table[region], in_part[pl.ds(region * ghost_rows, ghost_rows), :]
+    total = local[...]
+    for group in (back_near[:2], back_near[2:]):
+        for region in group:
+
+            @pl.when(exists(me + offsets[region]))
+            def _():
+                part_copy(region, me + offsets[region]).wait_recv()
+
+        total = total + sum(
+            mul(mirror_table[region], in_part[part_rows(region), :]) for region in group
         )
-        if region == order[-1]:
-            result_ref[...] = value
-        else:
-            local[...] = value
+    result_ref[...] = total
 
     for region, offset in enumerate(offsets):
 
@@ -328,6 +342,7 @@
             pltpu.VMEM((width, owned_rows), jnp.bfloat16),
             pltpu.VMEM((owned_rows, width), jnp.float32),
             pltpu.VMEM((column_total, elem_rows), jnp.bfloat16),
+            pltpu.VMEM((region_count, elem_rows, ghost_rows), jnp.bfloat16),
             pltpu.VMEM((width, elem_rows), jnp.float32),
             pltpu.VMEM((width, elem_rows), jnp.bfloat16),
             pltpu.VMEM((region_count, owned_rows, ghost_rows), jnp.bfloat16),

time: 18.8 us -> 16.7 us (0.89)
  Pallas kernels: 17.2 us -> 15.1 us
    pallas_call x1, Pallas kernels: 17.2 us -> 15.1 us  [per_device(): pl.pallas_call(functools.partial(kernel, n_curve, n_seg, ghost_rows, regi...]
where the time goes in v2:
time: 16.7 us; the launch traced here: 16.5 us
  Pallas kernels  15.1 us (90%)
  local copies, waits for them, and re-layouts  0.71 us (4%)
  between operations  0.66 us (4%)
    pallas_call x1, Pallas kernels, per_device(): pl.pallas_call(functools.partial(kernel, n_curve, n_seg, ghost_rows, regi...  15.1 us
    unnamed x1, local copies, waits for them, and re-layouts  0.71 us

profile of v2, /device:TPU:1, one launch (start us, length us, event | category | flops | bytes accessed | tf_op | source)
XLA Modules:
  0.0 16.5 jit_solution(13018225057718518093)
XLA Ops:
  0.7 15.1 %stokes_operator.1 = f32[512,128]{1,0:T(8,128)S(1)} custom-call(bf16[512,128]{1,0:T(8,128)(2,1)} %sol_in.1, f32[1,4096]{1,0:T(1,128)} %bitcast.6, s32[4,4096]{1,0:T(4,128)} %bitcast.4, s32[4,4096]{1,0:T(4,128)} %bitcast.5, s32[4,192]{1,0:T(4,128)} %bitcast.7, s32[1,4]{1,0:T(1,128)} %live_in.1, s32[1]{0:T(128)S(6)} %copy.12.count_in, ...), custom_call_target="tpu_custom_call" | custom-call | tf_op jit(solution)/shard_map/stokes_operator/pallas_call | solution.py:326
  15.7 0.7 %copy.11 = f32[512,128]{1,0:T(8,128)} copy(f32[512,128]{1,0:T(8,128)S(1)} %stokes_operator.1) | data formatting | bytes 524288

commit v3 on v2

--- a/solution.py
+++ b/solution.py
@@ -75,13 +75,6 @@
         (pres_mat_in, pres_mat_ref),
         (visc_in, visc_ref),
     )
-    loads = [
-        pltpu.make_async_copy(source, target, load_sem.at[position])
-        for position, (source, target) in enumerate(pairs)
-    ]
-    for load in loads:
-        load.start()
-
     devices_all = n_curve * n_seg
     owned_rows, width = sol_ref.shape
     slot_total, elem_rows = index_ref.shape
@@ -98,7 +91,7 @@
         return (safe // n_seg, safe % n_seg)
 
     barrier = pltpu.get_barrier_semaphore()
-    for offset in offsets:
+    for offset in offsets[::-1]:
 
         @pl.when(exists(me + offset))
         def _():
@@ -108,6 +101,13 @@
                 device_id=place(me + offset),
                 device_id_type=pl.DeviceIdType.MESH,
             )
+
+    loads = [
+        pltpu.make_async_copy(source, target, load_sem.at[position])
+        for position, (source, target) in enumerate(pairs)
+    ]
+    for load in loads:
+        load.start()
 
     for load in loads[:3]:
         load.wait()
@@ -138,15 +138,29 @@
     def part_rows(region):
         return pl.ds(pl.multiple_of(region * ghost_rows, GROUP), ghost_rows)
 
+    regions = list(range(region_count))
     edge = me < n_seg
-
-    def send_order(step_of):
-        near = sorted(range(region_count), key=lambda region: (abs(step_of(region)), step_of(region)))
-        down = sorted(range(region_count), key=step_of)
-        return near, [jnp.where(edge, first, other) for first, other in zip(down, near)]
-
-    near_order, order = send_order(lambda region: offsets[region])
-    back_near, back_order = send_order(lambda region: -offsets[region])
+    odd = me % 2 == 1
+    near_order = sorted(regions, key=lambda region: (abs(offsets[region]), offsets[region]))
+    down_order = sorted(regions, key=lambda region: offsets[region])
+    order = [jnp.where(edge, *pair) for pair in zip(down_order, near_order)]
+
+    def back_key(partner, by_step):
+        def key(region):
+            step = -offsets[region]
+            return (step == partner, step if by_step else abs(step), step)
+
+        return key
+
+    even_rest, odd_rest, even_edge, odd_edge = (
+        sorted(regions, key=back_key(partner, by_step))
+        for by_step in (False, True)
+        for partner in (1, -1)
+    )
+    back_order = [
+        jnp.where(edge, jnp.where(odd, first, second), jnp.where(odd, third, fourth))
+        for first, second, third, fourth in zip(odd_edge, even_edge, odd_rest, even_rest)
+    ]
 
     def ghost_copy(region, target):
         rows = part_rows(region)
@@ -245,16 +259,17 @@
             table_flip[region, columns, :] = table[pl.ds(first, ghost_rows), columns].T
 
     values = [gathered[:, columns] for columns in chunks]
-    for region in near_order:
-
-        @pl.when(exists(me - offset_of(region)))
-        def _():
-            ghost_copy(region, me - offset_of(region)).wait_recv()
-
-        flipped = in_ghost[part_rows(region), :].T
-        first = owned_rows + region * ghost_rows
+    for group in (near_order,):
+        for region in group:
+
+            @pl.when(exists(me - offset_of(region)))
+            def _():
+                ghost_copy(region, me - offset_of(region)).wait_recv()
+
+        first, count = min(group) * ghost_rows, len(group) * ghost_rows
+        flipped = in_ghost[pl.ds(first, count), :].T
         values = [
-            value + mul(flipped, table[pl.ds(first, ghost_rows), columns])
+            value + mul(flipped, table[pl.ds(owned_rows + first, count), columns])
             for value, columns in zip(values, chunks)
         ]
     pairs = []
@@ -265,30 +280,43 @@
     for pair, columns in zip(pairs, chunks):
         elem_out[:, columns] = mul(applied, pair).astype(jnp.bfloat16)
 
-    for group in (back_order[:2], back_order[2:]):
-        parts = [mul(elem_out[...], table_flip[region]) for region in group]
-        for region, part in zip(group, parts):
-            out_part[part_rows(region), :] = part.T.astype(jnp.bfloat16)
-        for region in group:
-
-            @pl.when(exists(me - offset_of(region)))
-            def _():
-                part_copy(region, me - offset_of(region)).start()
+    half = elem_rows // 2
+
+    def scatter(region):
+        return [
+            mul(elem_out[:, rows], table_flip[region, rows, :])
+            for rows in (pl.ds(0, half), pl.ds(half, half))
+        ]
+
+    coming = scatter(back_order[0])
+    for turn, region in enumerate(back_order):
+        front, back = coming
+        if turn < region_count - 1:
+            coming = scatter(back_order[turn + 1])
+        out_part[part_rows(region), :] = (front.T + back.T).astype(jnp.bfloat16)
+
+        @pl.when(exists(me - offset_of(region)))
+        def _():
+            part_copy(region, me - offset_of(region)).start()
 
     local[...] = mul(elem_out[...], table[pl.ds(0, owned_rows), :], NT).T
 
-    total = local[...]
-    for group in (back_near[:2], back_near[2:]):
+    halves = [pl.ds(first, owned_rows // 2) for first in (0, owned_rows // 2)]
+    totals = [local[rows, :] for rows in halves]
+    for group in (regions[:2], regions[2:]):
         for region in group:
 
             @pl.when(exists(me + offsets[region]))
             def _():
                 part_copy(region, me + offsets[region]).wait_recv()
 
-        total = total + sum(
-            mul(mirror_table[region], in_part[part_rows(region), :]) for region in group
-        )
-    result_ref[...] = total
+        totals = [
+            total
+            + sum(mul(mirror_table[region, rows, :], in_part[part_rows(region), :]) for region in group)
+            for total, rows in zip(totals, halves)
+        ]
+    for total, rows in zip(totals, halves):
+        result_ref[rows, :] = total
 
     for region, offset in enumerate(offsets):
 

time: 16.7 us -> 15.5 us (0.928)
  Pallas kernels: 15.1 us -> 13.9 us
    pallas_call x1, Pallas kernels: 15.1 us -> 13.9 us  [per_device(): pl.pallas_call(functools.partial(kernel, n_curve, n_seg, ghost_rows, regi...]
where the time goes in v3:
time: 15.5 us; the launch traced here: 15.3 us
  Pallas kernels  13.9 us (90%)
  local copies, waits for them, and re-layouts  0.71 us (5%)
  between operations  0.66 us (4%)
    pallas_call x1, Pallas kernels, per_device(): pl.pallas_call(functools.partial(kernel, n_curve, n_seg, ghost_rows, regi...  13.9 us
    unnamed x1, local copies, waits for them, and re-layouts  0.71 us

profile of v3, /device:TPU:1, one launch (start us, length us, event | category | flops | bytes accessed | tf_op | source)
XLA Modules:
  0.0 15.3 jit_solution(11689142049988207752)
XLA Ops:
  0.7 13.9 %stokes_operator.1 = f32[512,128]{1,0:T(8,128)S(1)} custom-call(bf16[512,128]{1,0:T(8,128)(2,1)} %sol_in.1, f32[1,4096]{1,0:T(1,128)} %bitcast.6, s32[4,4096]{1,0:T(4,128)} %bitcast.4, s32[4,4096]{1,0:T(4,128)} %bitcast.5, s32[4,192]{1,0:T(4,128)} %bitcast.7, s32[1,4]{1,0:T(1,128)} %live_in.1, s32[1]{0:T(128)S(6)} %copy.12.count_in, ...), custom_call_target="tpu_custom_call" | custom-call | tf_op jit(solution)/shard_map/stokes_operator/pallas_call | solution.py:354
  14.6 0.7 %copy.11 = f32[512,128]{1,0:T(8,128)} copy(f32[512,128]{1,0:T(8,128)S(1)} %stokes_operator.1) | data formatting | bytes 524288

commit v4 on v3

--- a/solution.py
+++ b/solution.py
@@ -10,6 +10,8 @@
 CHUNK = 1024
 GROUP = 16
 BLOCK = 64
+TILE = 256
+HEAD = 128
 NN = (((1,), (0,)), ((), ()))
 NT = (((1,), (1,)), ((), ()))
 TN = (((0,), (0,)), ((), ()))
@@ -109,8 +111,46 @@
     for load in loads:
         load.start()
 
-    for load in loads[:3]:
+    for load in loads[:6]:
         load.wait()
+
+    def table_rows(start, total, indices, weights):
+        shape = (total // GROUP, GROUP, chunk)
+        position = (
+            lax.broadcasted_iota(jnp.int32, shape, 0) * GROUP
+            + lax.broadcasted_iota(jnp.int32, shape, 1)
+            + start
+        ).astype(jnp.int16)
+        value = jnp.zeros(shape, jnp.bfloat16)
+        for index, weight in zip(indices, weights):
+            hit = position == jnp.broadcast_to(index[None], shape)
+            value = jnp.where(hit, jnp.broadcast_to(weight[None], shape), value)
+        return value.reshape(total, chunk)
+
+    chunks = [pl.ds(first, chunk) for first in range(0, elem_rows, chunk)]
+
+    def prepare(step, columns):
+        element = lax.broadcasted_iota(jnp.int32, (1, chunk), 1) + step * chunk
+        alive = element < count_ref[0]
+        indices, weights = [], []
+        for slot in range(slot_total):
+            index = index_ref[slot : slot + 1, columns]
+            code = code_ref[slot : slot + 1, columns].astype(jnp.float32) * 0.125
+            weight = jnp.where(alive, code, 0.0)
+            indices.append(jnp.broadcast_to(index, (GROUP, chunk)).astype(jnp.int16))
+            weights.append(jnp.broadcast_to(weight, (GROUP, chunk)).astype(jnp.bfloat16))
+        sums = []
+        for slot in range(slot_total):
+            value = weights[slot]
+            for other in range(slot):
+                same = indices[other] == indices[slot]
+                value = value + jnp.where(same, weights[other], jnp.zeros_like(value))
+            sums.append(value)
+        return indices, sums
+
+    def fill_owned(columns, first, last, ready):
+        for start in range(first, last, BLOCK):
+            table[pl.ds(start, BLOCK), columns] = table_rows(start, BLOCK, *ready)
 
     sol_flip[...] = sol_ref[...].T
 
@@ -132,6 +172,9 @@
             sol_flip[...], mirror_table[region]
         ).T.astype(jnp.bfloat16)
 
+    prepared = prepare(0, chunks[0])
+    fill_owned(chunks[0], 0, HEAD, prepared)
+
     def offset_of(region):
         return (region // 2 + 1) * (1 - 2 * (region % 2))
 
@@ -140,71 +183,80 @@
 
     regions = list(range(region_count))
     edge = me < n_seg
-    odd = me % 2 == 1
-    near_order = sorted(regions, key=lambda region: (abs(offsets[region]), offsets[region]))
-    down_order = sorted(regions, key=lambda region: offsets[region])
-    order = [jnp.where(edge, *pair) for pair in zip(down_order, near_order)]
-
-    def back_key(partner, by_step):
-        def key(region):
-            step = -offsets[region]
-            return (step == partner, step if by_step else abs(step), step)
-
-        return key
-
-    even_rest, odd_rest, even_edge, odd_edge = (
-        sorted(regions, key=back_key(partner, by_step))
-        for by_step in (False, True)
-        for partner in (1, -1)
-    )
-    back_order = [
-        jnp.where(edge, jnp.where(odd, first, second), jnp.where(odd, third, fourth))
-        for first, second, third, fourth in zip(odd_edge, even_edge, odd_rest, even_rest)
-    ]
-
-    def ghost_copy(region, target):
-        rows = part_rows(region)
+    odd = me % 2
+    incoming = [1 - odd, odd] + regions[2:]
+    outgoing = [odd, 1 - odd] + regions[2:]
+    lead = -ghost_rows % TILE
+    early = ghost_rows + lead
+    pieces = [(0, 0, ghost_rows), (1, 0, lead), (1, lead, ghost_rows - lead)]
+    pieces += [(slot, 0, ghost_rows) for slot in regions[2:]]
+
+    def piece_copy(number):
+        slot, first, count = pieces[number]
+        source = pl.multiple_of(outgoing[slot] * ghost_rows + first, GROUP)
         return pltpu.make_async_remote_copy(
-            src_ref=out_ghost.at[rows],
-            dst_ref=in_ghost.at[rows],
-            send_sem=send_sem.at[region],
-            recv_sem=recv_sem.at[region],
-            device_id=place(target),
+            src_ref=out_ghost.at[pl.ds(source, count)],
+            dst_ref=in_ghost.at[pl.ds(slot * ghost_rows + first, count)],
+            send_sem=send_sem.at[number],
+            recv_sem=recv_sem.at[number],
+            device_id=place(me + offset_of(outgoing[slot])),
             device_id_type=pl.DeviceIdType.MESH,
         )
 
-    def part_copy(region, target):
-        rows = part_rows(region)
+    def has_target(number):
+        return exists(me + offset_of(outgoing[pieces[number][0]]))
+
+    def has_source(number):
+        return exists(me - offset_of(incoming[pieces[number][0]]))
+
+    def incoming_of(slot):
+        return jnp.where(slot < 2, (1 - slot) * (1 - odd) + slot * odd, slot)
+
+    def part_copy(slot):
+        region = incoming_of(slot)
         return pltpu.make_async_remote_copy(
-            src_ref=out_part.at[rows],
-            dst_ref=in_part.at[rows],
+            src_ref=out_part.at[part_rows(slot)],
+            dst_ref=in_part.at[part_rows(region)],
+            send_sem=send_back_sem.at[slot],
+            recv_sem=recv_back_sem.at[region],
+            device_id=place(me - offset_of(region)),
+            device_id_type=pl.DeviceIdType.MESH,
+        )
+
+    def part_arrival(region):
+        return pltpu.make_async_remote_copy(
+            src_ref=out_part.at[part_rows(region)],
+            dst_ref=in_part.at[part_rows(region)],
             send_sem=send_back_sem.at[region],
             recv_sem=recv_back_sem.at[region],
-            device_id=place(target),
+            device_id=place(me + offsets[region]),
             device_id_type=pl.DeviceIdType.MESH,
         )
 
     peers = sum(jnp.where(exists(me + offset), 1, 0) for offset in offsets)
     pl.semaphore_wait(barrier, peers)
 
-    for region in order:
-
-        @pl.when(exists(me + offset_of(region)))
-        def _():
-            ghost_copy(region, me + offset_of(region)).start()
+    for number in (1, 0, 2, *range(len(pieces) - 1, 2, -1)):
+
+        @pl.when(has_target(number))
+        def _():
+            piece_copy(number).start()
+
+    for number, (slot, first, count) in enumerate(pieces):
+
+        @pl.when(jnp.logical_not(has_source(number)))
+        def _():
+            in_ghost[pl.ds(slot * ghost_rows + first, count), :] = jnp.zeros(
+                (count, width), jnp.bfloat16
+            )
 
     for region, offset in enumerate(offsets):
-        rows = pl.ds(region * ghost_rows, ghost_rows)
-
-        @pl.when(jnp.logical_not(exists(me - offset)))
-        def _():
-            in_ghost[rows, :] = jnp.zeros((ghost_rows, width), jnp.bfloat16)
 
         @pl.when(jnp.logical_not(exists(me + offset)))
         def _():
-            in_part[rows, :] = jnp.zeros((ghost_rows, width), jnp.bfloat16)
-
-    for load in loads[3:]:
+            in_part[part_rows(region), :] = jnp.zeros((ghost_rows, width), jnp.bfloat16)
+
+    for load in loads[6:]:
         load.wait()
 
     applied = jnp.concatenate(
@@ -215,58 +267,30 @@
         axis=1,
     )
 
-    def table_rows(start, total, indices, weights):
-        shape = (total // GROUP, GROUP, chunk)
-        position = (
-            lax.broadcasted_iota(jnp.int32, shape, 0) * GROUP
-            + lax.broadcasted_iota(jnp.int32, shape, 1)
-            + start
-        ).astype(jnp.int16)
-        value = jnp.zeros(shape, jnp.bfloat16)
-        for index, weight in zip(indices, weights):
-            hit = position == jnp.broadcast_to(index[None], shape)
-            value = jnp.where(hit, jnp.broadcast_to(weight[None], shape), value)
-        return value.reshape(total, chunk)
-
-    chunks = [pl.ds(first, chunk) for first in range(0, elem_rows, chunk)]
-
     for step, columns in enumerate(chunks):
-        element = lax.broadcasted_iota(jnp.int32, (1, chunk), 1) + step * chunk
-        alive = element < count_ref[0]
-        indices, weights = [], []
-        for slot in range(slot_total):
-            index = index_ref[slot : slot + 1, columns]
-            code = code_ref[slot : slot + 1, columns].astype(jnp.float32) * 0.125
-            weight = jnp.where(alive, code, 0.0)
-            indices.append(jnp.broadcast_to(index, (GROUP, chunk)).astype(jnp.int16))
-            weights.append(jnp.broadcast_to(weight, (GROUP, chunk)).astype(jnp.bfloat16))
-        sums = []
-        for slot in range(slot_total):
-            value = weights[slot]
-            for other in range(slot):
-                same = indices[other] == indices[slot]
-                value = value + jnp.where(same, weights[other], jnp.zeros_like(value))
-            sums.append(value)
-        for start in range(0, owned_rows, BLOCK):
-            table[pl.ds(start, BLOCK), columns] = table_rows(start, BLOCK, indices, sums)
+        indices, sums = ready = prepared if step == 0 else prepare(step, columns)
+        fill_owned(columns, HEAD if step == 0 else 0, owned_rows, ready)
         gathered[:, columns] = mul(sol_flip[...], table[pl.ds(0, owned_rows), columns])
-        for start in range(owned_rows, owned_rows + ghost_all, BLOCK):
-            table[pl.ds(start, BLOCK), columns] = table_rows(
-                start, BLOCK, indices[1:], sums[1:]
-            )
-        for region in range(region_count):
-            first = owned_rows + region * ghost_rows
-            table_flip[region, columns, :] = table[pl.ds(first, ghost_rows), columns].T
+        for slot in regions:
+            first = owned_rows + slot * ghost_rows
+            base = owned_rows + incoming[slot] * ghost_rows
+            for start in range(0, ghost_rows, BLOCK):
+                table[pl.ds(first + start, BLOCK), columns] = table_rows(
+                    base + start, BLOCK, indices[1:], sums[1:]
+                )
+            table_flip[slot, columns, :] = table[pl.ds(first, ghost_rows), columns].T
 
     values = [gathered[:, columns] for columns in chunks]
-    for group in (near_order,):
-        for region in group:
-
-            @pl.when(exists(me - offset_of(region)))
+    for group, first, count in (
+        ((0, 1), 0, early),
+        (range(2, len(pieces)), early, ghost_all - early),
+    ):
+        for number in group:
+
+            @pl.when(has_source(number))
             def _():
-                ghost_copy(region, me - offset_of(region)).wait_recv()
-
-        first, count = min(group) * ghost_rows, len(group) * ghost_rows
+                piece_copy(number).wait_recv()
+
         flipped = in_ghost[pl.ds(first, count), :].T
         values = [
             value + mul(flipped, table[pl.ds(owned_rows + first, count), columns])
@@ -288,27 +312,28 @@
             for rows in (pl.ds(0, half), pl.ds(half, half))
         ]
 
+    back_order = [jnp.where(edge, 2, 1), jnp.where(edge, 1, 2)] + regions[3:] + [0]
     coming = scatter(back_order[0])
-    for turn, region in enumerate(back_order):
+    for turn, slot in enumerate(back_order):
         front, back = coming
         if turn < region_count - 1:
             coming = scatter(back_order[turn + 1])
-        out_part[part_rows(region), :] = (front.T + back.T).astype(jnp.bfloat16)
-
-        @pl.when(exists(me - offset_of(region)))
-        def _():
-            part_copy(region, me - offset_of(region)).start()
+        out_part[part_rows(slot), :] = (front.T + back.T).astype(jnp.bfloat16)
+
+        @pl.when(exists(me - offset_of(incoming_of(slot))))
+        def _():
+            part_copy(slot).start()
 
     local[...] = mul(elem_out[...], table[pl.ds(0, owned_rows), :], NT).T
 
     halves = [pl.ds(first, owned_rows // 2) for first in (0, owned_rows // 2)]
     totals = [local[rows, :] for rows in halves]
-    for group in (regions[:2], regions[2:]):
+    for group in (regions[:2], regions[2:3], regions[3:]):
         for region in group:
 
             @pl.when(exists(me + offsets[region]))
             def _():
-                part_copy(region, me + offsets[region]).wait_recv()
+                part_arrival(region).wait_recv()
 
         totals = [
             total
@@ -318,15 +343,17 @@
     for total, rows in zip(totals, halves):
         result_ref[rows, :] = total
 
-    for region, offset in enumerate(offsets):
-
-        @pl.when(exists(me + offset))
-        def _():
-            ghost_copy(region, me + offset).wait_send()
-
-        @pl.when(exists(me - offset))
-        def _():
-            part_copy(region, me - offset).wait_send()
+    for number in range(len(pieces)):
+
+        @pl.when(has_target(number))
+        def _():
+            piece_copy(number).wait_send()
+
+    for slot in regions:
+
+        @pl.when(exists(me - offset_of(incoming_of(slot))))
+        def _():
+            part_copy(slot).wait_send()
 
 
 def per_device(
@@ -351,6 +378,7 @@
     hbm = pl.BlockSpec(memory_space=pltpu.HBM)
     ghost_buffer = pltpu.VMEM((ghost_all, width), jnp.bfloat16)
     semaphores = pltpu.SemaphoreType.DMA((region_count,))
+    piece_semaphores = pltpu.SemaphoreType.DMA((region_count + 1,))
     return pl.pallas_call(
         functools.partial(kernel, n_curve, n_seg, ghost_rows, region_count),
         out_shape=pltpu.VMEM((owned_rows, width), jnp.float32),
@@ -378,8 +406,8 @@
             ghost_buffer,
             ghost_buffer,
             ghost_buffer,
-            semaphores,
-            semaphores,
+            piece_semaphores,
+            piece_semaphores,
             semaphores,
             semaphores,
         ],

time: 15.5 us -> 15.2 us (0.981)
  Pallas kernels: 13.9 us -> 13.7 us
    pallas_call x1, Pallas kernels: 13.9 us -> 13.7 us  [per_device(): pl.pallas_call(functools.partial(kernel, n_curve, n_seg, ghost_rows, regi...]
where the time goes in v4:
time: 15.2 us; the launch traced here: 15.1 us
  Pallas kernels  13.7 us (90%)
  local copies, waits for them, and re-layouts  0.71 us (5%)
  between operations  0.66 us (4%)
    pallas_call x1, Pallas kernels, per_device(): pl.pallas_call(functools.partial(kernel, n_curve, n_seg, ghost_rows, regi...  13.7 us
    unnamed x1, local copies, waits for them, and re-layouts  0.71 us

profile of v4, /device:TPU:1, one launch (start us, length us, event | category | flops | bytes accessed | tf_op | source)
XLA Modules:
  0.0 15.1 jit_solution(14768498174121293658)
XLA Ops:
  0.7 13.7 %stokes_operator.1 = f32[512,128]{1,0:T(8,128)S(1)} custom-call(bf16[512,128]{1,0:T(8,128)(2,1)} %sol_in.1, f32[1,4096]{1,0:T(1,128)} %bitcast.6, s32[4,4096]{1,0:T(4,128)} %bitcast.4, s32[4,4096]{1,0:T(4,128)} %bitcast.5, s32[4,192]{1,0:T(4,128)} %bitcast.7, s32[1,4]{1,0:T(1,128)} %live_in.1, s32[1]{0:T(128)S(6)} %copy.12.count_in, ...), custom_call_target="tpu_custom_call" | custom-call | tf_op jit(solution)/shard_map/stokes_operator/pallas_call | solution.py:382
  14.3 0.7 %copy.11 = f32[512,128]{1,0:T(8,128)} copy(f32[512,128]{1,0:T(8,128)S(1)} %stokes_operator.1) | data formatting | bytes 524288

commit v5 on v4

--- a/solution.py
+++ b/solution.py
@@ -236,7 +236,7 @@
     peers = sum(jnp.where(exists(me + offset), 1, 0) for offset in offsets)
     pl.semaphore_wait(barrier, peers)
 
-    for number in (1, 0, 2, *range(len(pieces) - 1, 2, -1)):
+    for number in (1, 2, *range(len(pieces) - 1, 2, -1), 0):
 
         @pl.when(has_target(number))
         def _():

time: 15.2 us -> 15.2 us (level)
  no operation moved by 1% of the time
where the time goes in v5:
time: 15.2 us; the launch traced here: 15.1 us
  Pallas kernels  13.7 us (90%)
  local copies, waits for them, and re-layouts  0.71 us (5%)
  between operations  0.66 us (4%)
    pallas_call x1, Pallas kernels, per_device(): pl.pallas_call(functools.partial(kernel, n_curve, n_seg, ghost_rows, regi...  13.7 us
    unnamed x1, local copies, waits for them, and re-layouts  0.71 us

profile of v5, /device:TPU:1, one launch (start us, length us, event | category | flops | bytes accessed | tf_op | source)
XLA Modules:
  0.0 15.1 jit_solution(7706226018959187296)
XLA Ops:
  0.7 13.7 %stokes_operator.1 = f32[512,128]{1,0:T(8,128)S(1)} custom-call(bf16[512,128]{1,0:T(8,128)(2,1)} %sol_in.1, f32[1,4096]{1,0:T(1,128)} %bitcast.6, s32[4,4096]{1,0:T(4,128)} %bitcast.4, s32[4,4096]{1,0:T(4,128)} %bitcast.5, s32[4,192]{1,0:T(4,128)} %bitcast.7, s32[1,4]{1,0:T(1,128)} %live_in.1, s32[1]{0:T(128)S(6)} %copy.12.count_in, ...), custom_call_target="tpu_custom_call" | custom-call | tf_op jit(solution)/shard_map/stokes_operator/pallas_call | solution.py:382
  14.3 0.7 %copy.11 = f32[512,128]{1,0:T(8,128)} copy(f32[512,128]{1,0:T(8,128)S(1)} %stokes_operator.1) | data formatting | bytes 524288
